TPU v7x, 32 devices: a whole 2x2x4 slice. The times are simulated.
32 devices in a mesh: fsdp: 8 (over z, y), rep: 4 (over x, core).
Axes of the slice: x: 2, y: 2, z: 4, core: 2. Of those that a mesh axis runs over, the one named last changes fastest.
Arguments:
- partial_grad: bfloat16 [4, 8, 1024, 1024], P('rep', None, 'fsdp'), may hold values from -3 to 3
- owner_table: int32 [8, 2], replicated, may hold values from -1 to 7, as said below
- left_stat: float32 [8, 2, 1024, 1024], P('fsdp', None, None, 'rep'), may hold values from -6 to 6
- right_stat: float32 [8, 2, 1024, 1024], P('fsdp', None, None, 'rep'), may hold values from -6 to 6
- left_root: bfloat16 [8, 2, 1024, 1024], P('fsdp', None, None, 'rep'), may hold values from -0.1875 to 0.1875
- right_root: bfloat16 [8, 2, 1024, 1024], P('fsdp', None, None, 'rep'), may hold values from -0.1875 to 0.1875
Outputs:
- left_new: float32 [8, 2, 1024, 1024], P('fsdp', None, None, 'rep')
- right_new: float32 [8, 2, 1024, 1024], P('fsdp', None, None, 'rep')
- update: bfloat16 [8, 1024, 1024], P(None, 'fsdp', 'rep')
Inputs may be any that keep to these rules, and one draw needn't show every extreme that they name: `owner_table`: each of the 8 blocks stands in exactly one slot and -1 marks an empty slot; some owner fills all 2 slots and some owner has none.
All inputs are finite; a program needn't handle non-finite values.
Results may differ from a plain program's by a relative error of at most 0.014.
Values may be sent and summed in bfloat16 or wider, within the bound.
No kernel may reach another device: no remote copies, remote signals or barrier semaphores. Data moves between devices by JAX's collectives and lax.ppermute only.
A program may use at most 64 MiB of HBM per device.

v0:
```python
import functools

import jax
import jax.numpy as jnp
from jax import lax
from jax.experimental import pallas as pl
from jax.experimental.pallas import tpu as pltpu
from jax.sharding import PartitionSpec as P


decay_rate = 0.99


def pair_kernel(where_ref, mine_ref, near_ref, *outs):
    width = mine_ref.shape[2]
    cols = pl.ds(pl.multiple_of((where_ref[1] ^ 2) * width, width), width)
    total = (mine_ref[...].astype(jnp.float32) + near_ref[:, :, cols].astype(jnp.float32)).astype(jnp.bfloat16)
    for p in range(2):
        outs[p][...] = total[:, :, p * width // 2 : (p + 1) * width // 2]


def base_kernel(where_ref, grad_ref, near_ref, out_ref):
    width = out_ref.shape[3]
    for q in range(2):
        cols = pl.ds(pl.multiple_of((where_ref[1] ^ q) * width, width), width)
        out_ref[q] = grad_ref[:, :, cols].astype(jnp.float32) + near_ref[:, :, cols].astype(jnp.float32)


def route_kernel(wanted, table_ref, where_ref, base_ref, *refs):
    sums, pieces = refs[: len(refs) - len(wanted)], refs[len(refs) - len(wanted) :]
    me, side = where_ref[0], where_ref[1] & 1
    step = sums[0].shape[2]
    for (k, parts), piece in zip(wanted, pieces):
        block = table_ref[(me ^ k) * 2 + side]

        @pl.when(block >= 0)
        def _(parts=parts, piece=piece, block=block):
            for n, p in enumerate(parts):
                for q in range(2):
                    total = base_ref[q, block, :, p * step : (p + 1) * step]
                    far_ref = sums[2 * p + q] if len(sums) > 2 else sums[q]
                    total = total + far_ref[block].astype(jnp.float32)
                    piece[side ^ q, :, n * step : (n + 1) * step] = total.astype(jnp.bfloat16)

        @pl.when(block < 0)
        def _(piece=piece):
            piece[...] = jnp.zeros(piece.shape, jnp.bfloat16)


def join_kernel(*refs):
    for n in range(len(refs) - 1):
        refs[-1][n] = refs[n][...]


def product_kernel(owners, where_ref, *refs):
    joined_ref, right_ref, beside_ref, grad_ref, prod_ref = refs[-5:]
    half = owners // 2
    rows, width = refs[0].shape[1:]
    step = width // 2
    me, side, place = where_ref[0], where_ref[1] & 1, where_ref[1] >> 1
    for k in range(owners):
        first = pl.ds(pl.multiple_of((me ^ k) * rows, rows), rows)
        for i in range(2):
            for q in range(2):
                col = pl.multiple_of(((place ^ i) * 2 + q) * width, width)
                if k < half:
                    grad_ref[first, pl.ds(col, width)] = refs[2 * k + i][q]
                else:
                    early = joined_ref[k - half, q] if i else refs[2 * owners + k - half][q]
                    grad_ref[first, pl.ds(col, step)] = early
                    grad_ref[first, pl.ds(pl.multiple_of(col + step, step), step)] = refs[2 * k + i][q]
    for i, right in enumerate((right_ref[side], beside_ref[...])):
        prod_ref[i] = jnp.dot(grad_ref[...], right, preferred_element_type=jnp.float32).astype(jnp.bfloat16)


def apply_kernel(where_ref, near_ref, far_ref, prod_ref, even_ref, odd_ref):
    _, both, width = near_ref.shape
    rows = both // 2
    me, rep = where_ref[0], where_ref[1]
    side = rep & 1
    swapped = (me & 1) == 1
    for i in range(2):
        total = None
        for q in range(4):
            band = pl.ds(pl.multiple_of((rep ^ q) * width, width), width)
            ref = far_ref if q & 2 else near_ref
            term = jnp.dot(ref[q & 1], prod_ref[i, band, :], preferred_element_type=jnp.float32)
            total = term if total is None else total + term
        total = total.astype(jnp.bfloat16)
        even_ref[side ^ i] = jnp.where(swapped, total[rows:], total[:rows])
        odd_ref[side ^ i] = jnp.where(swapped, total[:rows], total[rows:])


def stats_kernel(table_ref, where_ref, grad_ref, other_ref, left_ref, right_ref, left_out, right_out):
    me, rep = where_ref[0], where_ref[1]
    _, _, width = left_ref.shape
    slot = pl.program_id(0)
    filled = table_ref[me * 2 + slot] >= 0
    share = pl.ds(pl.multiple_of(rep * width, width), width)

    def update(ref):
        rows, cols = ref[share, :], ref[:, share]
        left = lax.dot_general(ref[...], rows, (((1,), (1,)), ((), ())), preferred_element_type=jnp.float32)
        left_out[0] = decay_rate * left_ref[0] + (1.0 - decay_rate) * left
        right = lax.dot_general(cols, ref[...], (((0,), (0,)), ((), ())), preferred_element_type=jnp.float32)
        right_out[0] = decay_rate * right_ref[0] + (1.0 - decay_rate) * right.T

    @pl.when(filled & (slot == (rep & 1)))
    def _():
        update(grad_ref)

    @pl.when(filled & (slot != (rep & 1)))
    def _():
        update(other_ref)

    @pl.when(jnp.logical_not(filled))
    def _():
        left_out[...] = left_ref[...]
        right_out[...] = right_ref[...]


def stats(table, where, grad, other, left, right):
    whole = pl.BlockSpec(grad.shape, lambda i, *_: (0, 0))
    one = pl.BlockSpec((1,) + left.shape[1:], lambda i, *_: (i, 0, 0))
    return pl.pallas_call(
        stats_kernel,
        grid_spec=pltpu.PrefetchScalarGridSpec(
            num_scalar_prefetch=2,
            grid=(2,),
            in_specs=[whole, whole, one, one],
            out_specs=[one, one],
        ),
        out_shape=[jax.ShapeDtypeStruct(left.shape, left.dtype)] * 2,
        compiler_params=pltpu.CompilerParams(vmem_limit_bytes=28 * 1024 * 1024),
    )(table, where, grad, other, left, right)


def left_kernel(both, where_ref, left_ref, near_ref, *parts):
    me, side = where_ref[0], where_ref[1] & 1
    for j in range(len(parts)):
        rows = pl.ds(pl.multiple_of(((me >> 1) ^ j) * both, both), both)
        parts[j][0] = left_ref[side, rows, :]
        parts[j][1] = near_ref[rows, :]


def pack_kernel(owners, where_ref, *refs):
    for k in range(owners):
        refs[-1][k] = refs[k][1 - (where_ref[1] & 1)]


def collect_kernel(owners, table_ref, where_ref, *refs):
    pieces, beside_ref, out_ref = refs[:-2], refs[-2], refs[-1]
    me, side = where_ref[0], where_ref[1] & 1
    for k in range(owners):
        block = table_ref[(me ^ k) * 2 + side]

        @pl.when(block >= 0)
        def _(k=k, block=block):
            out_ref[block] = pieces[k][side]

        beside = table_ref[(me ^ k) * 2 + 1 - side]

        @pl.when(beside >= 0)
        def _(k=k, beside=beside):
            out_ref[beside] = beside_ref[k]


def call(kernel, scalars, out_shape, ins, scratch=()):
    vmem = pl.BlockSpec(memory_space=pltpu.VMEM)
    smem = pl.BlockSpec(memory_space=pltpu.SMEM)
    return pl.pallas_call(
        kernel,
        out_shape=out_shape,
        in_specs=[smem] * len(scalars) + [vmem] * len(ins),
        out_specs=jax.tree.map(lambda _: vmem, out_shape),
        scratch_shapes=scratch,
        compiler_params=pltpu.CompilerParams(vmem_limit_bytes=24 * 1024 * 1024),
    )(*scalars, *ins)


def on_device(owners, quarters, partial_grad, owner_table, left_stat, right_stat, left_root, right_root):
    grad = partial_grad[0]
    me, rep = lax.axis_index("fsdp"), lax.axis_index("rep")
    side = rep & 1
    slots, order, width = left_stat.shape[1:]
    assert slots == 2
    rows = grad.shape[1]
    table = owner_table.reshape(-1)
    where = jnp.stack([me, rep]).astype(jnp.int32)
    bf16 = lambda *shape: jax.ShapeDtypeStruct(shape, jnp.bfloat16)

    def swap(x, bits):
        return lax.ppermute(x, "rep", [(r, r ^ bits) for r in range(quarters)])

    def give(x, k):
        return lax.ppermute(x, "fsdp", [(f, f ^ k) for f in range(owners)])

    def slot(x, s):
        return lax.dynamic_index_in_dim(x, s, 0, keepdims=False)

    near = swap(grad, 1)
    part = lax.dynamic_slice_in_dim(grad, (rep ^ 2) * width, width, 2)
    halves = call(pair_kernel, (where,), (bf16(grad.shape[0], rows, width // 2),) * 2, (part, near))
    across = [swap(halves[p], 2) for p in range(2)]
    base = jax.ShapeDtypeStruct((2, *part.shape), jnp.float32)
    base = call(base_kernel, (where,), base, (grad, near))
    beside = [swap(across[p], 1) for p in range(2)]
    left, right = left_root[0], right_root[0]
    left_near = swap(slot(left, 1 - side), 1)
    right_near = swap(slot(right, 1 - side), 1)
    left_parts = call(
        functools.partial(left_kernel, 2 * rows),
        (where,),
        (bf16(2, 2 * rows, width),) * (owners // 2),
        (left, left_near),
    )
    half = owners // 2
    piece, split = bf16(2, rows, width), bf16(2, rows, width // 2)
    early = call(
        functools.partial(route_kernel, [(k, (0,)) for k in range(half, owners)]),
        (table, where),
        (split,) * half,
        (base, across[0], beside[0]),
    )
    pieces = call(
        functools.partial(route_kernel, [(k, (0, 1)) for k in range(half)] + [(k, (1,)) for k in range(half, owners)]),
        (table, where),
        (piece,) * half + (split,) * half,
        (base, across[0], beside[0], across[1], beside[1]),
    )
    early = [give(early[k - half], k) for k in range(half, owners)]
    joined = call(join_kernel, (), bf16(half, 2, rows, width // 2), early)
    joined = swap(joined, 2)
    gathered = []
    for k in range(owners):
        own = give(pieces[k], k) if k else pieces[k]
        gathered += [own, swap(own, 2)]
    gradient, product = call(
        functools.partial(product_kernel, owners),
        (where,),
        (bf16(order, order), bf16(2, order, width)),
        (*gathered, *early, joined, right, right_near),
    )
    returned = {}
    for j in reversed(range(owners // 2)):
        part = left_parts[j]
        far = swap(part, 2)
        same, odd = call(apply_kernel, (where,), (bf16(2, rows, width),) * 2, (part, far, product))
        returned[2 * j + 1] = give(odd, 2 * j + 1)
        returned[2 * j] = give(same, 2 * j) if j else same
    other = swap(gradient, 1)
    left_next, right_next = stats(table, where, gradient, other, left_stat[0], right_stat[0])
    returned[0], left_next, right_next = lax.optimization_barrier((returned[0], left_next, right_next))
    returned = [returned[k] for k in range(owners)]
    packed = call(functools.partial(pack_kernel, owners), (where,), bf16(owners, rows, width), returned)
    update = call(
        functools.partial(collect_kernel, owners),
        (table, where),
        bf16(grad.shape[0], rows, width),
        (*returned, swap(packed, 1)),
    )
    return left_next[None], right_next[None], update


def solution(mesh):
    owners, quarters = mesh.shape["fsdp"], mesh.shape["rep"]
    assert quarters == 4 and owners & (owners - 1) == 0
    stat = P("fsdp", None, None, "rep")

    def body(*args):
        return on_device(owners, quarters, *args)

    return jax.shard_map(
        body,
        mesh=mesh,
        in_specs=(P("rep", None, "fsdp", None), P(), stat, stat, stat, stat),
        out_specs=(stat, stat, P(None, "fsdp", "rep")),
        check_vma=False,
    )
```

profile of v0, /device:TPU:0, one launch (start us, length us, event | category | flops | bytes accessed | tf_op | source)
XLA Modules:
  0.0 129.5 jit_solution(1610626820291855105)
XLA Ops:
  2.4 2.8 %collective-permute-done.2.near_ref = bf16[8,128,1024]{2,1,0:T(8,128)(2,1)S(1)} collective-permute-done((bf16[8,128,1024]{2,1,0:T(8,128)(2,1)}, bf16[8,128,1024]{2,1,0:T(8,128)(2,1)S(1)}, u32[]{:S(2)}, u32[]{:S(2)}) %collective-permute-start.2) | collective-permute-done | bytes 2097184 | tf_op jit(solution)/shard_map/ppermute | solution.py:193
  5.9 2.9 %collective-permute-start.3 = (bf16[8,128,128]{2,1,0:T(8,128)(2,1)S(1)}, bf16[8,128,128]{2,1,0:T(8,128)(2,1)S(1)}, u32[]{:S(2)}, u32[]{:S(2)}) collective-permute-start(bf16[8,128,128]{2,1,0:T(8,128)(2,1)S(1)} %get-tuple-element.37), channel_id=1, source_target_pairs={{0,2},{1,3},{2,0},{3,1},{4,6},{5,7},{6,4},{7,5},{8,10},{9,11},{10,... | collective-permute-start | bytes 786440 | tf_op jit(solution)/shard_map/ppermute | solution.py:193
  9.7 6.2 %collective-permute-done.3.refs_0_ = bf16[8,128,128]{2,1,0:T(8,128)(2,1)S(1)} collective-permute-done((bf16[8,128,128]{2,1,0:T(8,128)(2,1)S(1)}, bf16[8,128,128]{2,1,0:T(8,128)(2,1)S(1)}, u32[]{:S(2)}, u32[]{:S(2)}) %collective-permute-start.3) | collective-permute-done | bytes 262176 | tf_op jit(solution)/shard_map/ppermute | solution.py:193
  16.0 5.2 %collective-permute-done.5.refs_2_ = bf16[8,128,128]{2,1,0:T(8,128)(2,1)} collective-permute-done((bf16[8,128,128]{2,1,0:T(8,128)(2,1)S(1)}, bf16[8,128,128]{2,1,0:T(8,128)(2,1)}, u32[]{:S(2)}, u32[]{:S(2)}) %collective-permute-start.5) | collective-permute-done | bytes 262176 | tf_op jit(solution)/shard_map/ppermute | solution.py:193
  24.8 2.9 %collective-permute-start.22 = (bf16[2,128,128]{2,1,0:T(8,128)(2,1)S(1)}, bf16[2,128,128]{2,1,0:T(8,128)(2,1)S(1)}, u32[]{:S(2)}, u32[]{:S(2)}) collective-permute-start(bf16[2,128,128]{2,1,0:T(8,128)(2,1)S(1)} %get-tuple-element.47), channel_id=1, source_target_pairs={{0,16},{4,20},{8,24},{12,28},{16,0},{20,4},{24,8},{28,12},{1,17},{... | collective-permute-start | bytes 196616 | tf_op jit(solution)/shard_map/ppermute | solution.py:196
  29.0 3.6 %collective-permute-start.24 = (bf16[2,128,128]{2,1,0:T(8,128)(2,1)S(1)}, bf16[2,128,128]{2,1,0:T(8,128)(2,1)S(1)}, u32[]{:S(2)}, u32[]{:S(2)}) collective-permute-start(bf16[2,128,128]{2,1,0:T(8,128)(2,1)S(1)} %get-tuple-element.49), channel_id=1, source_target_pairs={{0,24},{4,28},{8,16},{12,20},{16,8},{20,12},{24,0},{28,4},{1,25},{... | collective-permute-start | bytes 196616 | tf_op jit(solution)/shard_map/ppermute | solution.py:196
  34.1 2.8 %collective-permute-start.16 = (bf16[2,128,128]{2,1,0:T(8,128)(2,1)S(1)}, bf16[2,128,128]{2,1,0:T(8,128)(2,1)S(1)}, u32[]{:S(2)}, u32[]{:S(2)}) collective-permute-start(bf16[2,128,128]{2,1,0:T(8,128)(2,1)S(1)} %get-tuple-element.44), channel_id=1, source_target_pairs={{0,20},{4,16},{8,28},{12,24},{16,4},{20,0},{24,12},{28,8},{1,21},{... | collective-permute-start | bytes 196616 | tf_op jit(solution)/shard_map/ppermute | solution.py:196
  37.0 2.6 %collective-permute-done.23.refs_1_.refs_17_ = bf16[2,128,128]{2,1,0:T(8,128)(2,1)S(1)} collective-permute-done((bf16[2,128,128]{2,1,0:T(8,128)(2,1)S(1)}, bf16[2,128,128]{2,1,0:T(8,128)(2,1)S(1)}, u32[]{:S(2)}, u32[]{:S(2)}) %collective-permute-start.23) | collective-permute-done | bytes 65568 | tf_op jit(solution)/shard_map/ppermute | solution.py:196
  39.5 5.3 %collective-permute-start.25 = (bf16[2,128,128]{2,1,0:T(8,128)(2,1)S(1)}, bf16[2,128,128]{2,1,0:T(8,128)(2,1)S(1)}, u32[]{:S(2)}, u32[]{:S(2)}) collective-permute-start(bf16[2,128,128]{2,1,0:T(8,128)(2,1)S(1)} %get-tuple-element.50), channel_id=1, source_target_pairs={{0,28},{4,24},{8,20},{12,16},{16,12},{20,8},{24,4},{28,0},{1,29},{... | collective-permute-start | bytes 196616 | tf_op jit(solution)/shard_map/ppermute | solution.py:196
  50.0 1.8 %collective-permute-done.20.refs_14_ = bf16[2,128,128]{2,1,0:T(8,128)(2,1)S(1)} collective-permute-done((bf16[2,128,128]{2,1,0:T(8,128)(2,1)S(1)}, bf16[2,128,128]{2,1,0:T(8,128)(2,1)S(1)}, u32[]{:S(2)}, u32[]{:S(2)}) %collective-permute-start.20) | collective-permute-done | bytes 65568 | tf_op jit(solution)/shard_map/ppermute | solution.py:196
  55.8 7.1 %collective-permute-done.21.refs_15_ = bf16[2,128,128]{2,1,0:T(8,128)(2,1)S(1)} collective-permute-done((bf16[2,128,128]{2,1,0:T(8,128)(2,1)S(1)}, bf16[2,128,128]{2,1,0:T(8,128)(2,1)S(1)}, u32[]{:S(2)}, u32[]{:S(2)}) %collective-permute-start.21) | collective-permute-done | bytes 65568 | tf_op jit(solution)/shard_map/ppermute | solution.py:193
  66.9 2.3 %collective-permute-done.7.refs_1_ = bf16[2,128,256]{2,1,0:T(8,128)(2,1)S(1)} collective-permute-done((bf16[2,128,256]{2,1,0:T(8,128)(2,1)S(1)}, bf16[2,128,256]{2,1,0:T(8,128)(2,1)S(1)}, u32[]{:S(2)}, u32[]{:S(2)}) %collective-permute-start.7) | collective-permute-done | bytes 131104 | tf_op jit(solution)/shard_map/ppermute | solution.py:193
  69.2 2.8 %collective-permute-done.9.refs_3_ = bf16[2,128,256]{2,1,0:T(8,128)(2,1)S(1)} collective-permute-done((bf16[2,128,256]{2,1,0:T(8,128)(2,1)S(1)}, bf16[2,128,256]{2,1,0:T(8,128)(2,1)S(1)}, u32[]{:S(2)}, u32[]{:S(2)}) %collective-permute-start.9) | collective-permute-done | bytes 131104 | tf_op jit(solution)/shard_map/ppermute | solution.py:193
  72.0 1.9 %collective-permute-done.11.refs_5_ = bf16[2,128,256]{2,1,0:T(8,128)(2,1)S(1)} collective-permute-done((bf16[2,128,256]{2,1,0:T(8,128)(2,1)S(1)}, bf16[2,128,256]{2,1,0:T(8,128)(2,1)S(1)}, u32[]{:S(2)}, u32[]{:S(2)}) %collective-permute-start.11) | collective-permute-done | bytes 131104 | tf_op jit(solution)/shard_map/ppermute | solution.py:193
  75.3 2.7 %shard_map.91 = (bf16[1024,1024]{1,0:T(8,128)(2,1)S(1)}, bf16[2,1024,256]{2,1,0:T(8,128)(2,1)S(1)}) custom-call(s32[2]{0:T(128)S(1)} %pad_add_fusion.where_ref, bf16[2,128,256]{2,1,0:T(8,128)(2,1)S(1)} %get-tuple-element.39.refs_0_, bf16[2,128,256]{2,1,0:T(8,128)(2,1)S(1)} %collective-permute-done.7.refs_1_, ...), custom_call_target="tpu_custom_call" | custom-call | tf_op jit(solution)/shard_map/pallas_call | solution.py:171
  78.7 4.3 %collective-permute-done.near_ref = bf16[1024,256]{1,0:T(8,128)(2,1)S(1)} collective-permute-done((bf16[1024,256]{1,0:T(8,128)(2,1)S(1)}, bf16[1024,256]{1,0:T(8,128)(2,1)S(1)}, u32[]{:S(2)}, u32[]{:S(2)}) %collective-permute-start) | collective-permute-done | bytes 524320 | tf_op jit(solution)/shard_map/ppermute | solution.py:193
  87.7 5.1 %collective-permute-done.36.far_ref = bf16[2,256,256]{2,1,0:T(8,128)(2,1)S(1)} collective-permute-done((bf16[2,256,256]{2,1,0:T(8,128)(2,1)S(1)}, bf16[2,256,256]{2,1,0:T(8,128)(2,1)S(1)}, u32[]{:S(2)}, u32[]{:S(2)}) %collective-permute-start.36) | collective-permute-done | bytes 262176 | tf_op jit(solution)/shard_map/ppermute | solution.py:193
  93.8 3.5 %collective-permute-start.37 = (bf16[2,128,256]{2,1,0:T(8,128)(2,1)S(1)}, bf16[2,128,256]{2,1,0:T(8,128)(2,1)S(1)}, u32[]{:S(2)}, u32[]{:S(2)}) collective-permute-start(bf16[2,128,256]{2,1,0:T(8,128)(2,1)S(1)} %get-tuple-element.67), channel_id=1, source_target_pairs={{0,24},{4,28},{8,16},{12,20},{16,8},{20,12},{24,0},{28,4},{1,25},{... | collective-permute-start | bytes 393224 | tf_op jit(solution)/shard_map/ppermute | solution.py:196
  98.4 4.6 %collective-permute-start.38 = (bf16[2,128,256]{2,1,0:T(8,128)(2,1)S(1)}, bf16[2,128,256]{2,1,0:T(8,128)(2,1)S(1)}, u32[]{:S(2)}, u32[]{:S(2)}) collective-permute-start(bf16[2,128,256]{2,1,0:T(8,128)(2,1)S(1)} %get-tuple-element.68), channel_id=1, source_target_pairs={{0,28},{4,24},{8,20},{12,16},{16,12},{20,8},{24,4},{28,0},{1,29},{... | collective-permute-start | bytes 393224 | tf_op jit(solution)/shard_map/ppermute | solution.py:196
  104.0 3.4 %collective-permute-start.34 = (bf16[2,128,256]{2,1,0:T(8,128)(2,1)S(1)}, bf16[2,128,256]{2,1,0:T(8,128)(2,1)S(1)}, u32[]{:S(2)}, u32[]{:S(2)}) collective-permute-start(bf16[2,128,256]{2,1,0:T(8,128)(2,1)S(1)} %get-tuple-element.64), channel_id=1, source_target_pairs={{0,16},{4,20},{8,24},{12,28},{16,0},{20,4},{24,8},{28,12},{1,17},{... | collective-permute-start | bytes 393224 | tf_op jit(solution)/shard_map/ppermute | solution.py:196
  108.8 4.5 %collective-permute-start.35 = (bf16[2,128,256]{2,1,0:T(8,128)(2,1)S(1)}, bf16[2,128,256]{2,1,0:T(8,128)(2,1)S(1)}, u32[]{:S(2)}, u32[]{:S(2)}) collective-permute-start(bf16[2,128,256]{2,1,0:T(8,128)(2,1)S(1)} %get-tuple-element.65), channel_id=1, source_target_pairs={{0,20},{4,16},{8,28},{12,24},{16,4},{20,0},{24,12},{28,8},{1,21},{... | collective-permute-start | bytes 393224 | tf_op jit(solution)/shard_map/ppermute | solution.py:196
  117.9 4.7 %shard_map.93 = (f32[2,1024,256]{2,1,0:T(8,128)}, f32[2,1024,256]{2,1,0:T(8,128)}) custom-call(s32[16]{0:T(128)S(1)} %reshape.14.table_ref, s32[2]{0:T(128)S(1)} %pad_add_fusion.where_ref, bf16[1024,1024]{1,0:T(8,128)(2,1)S(1)} %get-tuple-element.53.grad_ref, bf16[1024,1024]{1,0:T(8,128)(2,1)S(1)} %collective-permute-done.28.other_ref, ...), custom_call_target="tpu_custom_call" | custom-call | tf_op jit(solution)/shard_map/pallas_call | solution.py:125
  122.6 2.6 %collective-permute-done.32.refs_3_ = bf16[2,128,256]{2,1,0:T(8,128)(2,1)S(1)} collective-permute-done((bf16[2,128,256]{2,1,0:T(8,128)(2,1)S(1)}, bf16[2,128,256]{2,1,0:T(8,128)(2,1)S(1)}, u32[]{:S(2)}, u32[]{:S(2)}) %collective-permute-start.32) | collective-permute-done | bytes 131104 | tf_op jit(solution)/shard_map/ppermute | solution.py:196
  126.0 1.9 %collective-permute-done.39.refs_8_ = bf16[8,128,256]{2,1,0:T(8,128)(2,1)S(1)} collective-permute-done((bf16[8,128,256]{2,1,0:T(8,128)(2,1)S(1)}, bf16[8,128,256]{2,1,0:T(8,128)(2,1)S(1)}, u32[]{:S(2)}, u32[]{:S(2)}) %collective-permute-start.39) | collective-permute-done | bytes 524320 | tf_op jit(solution)/shard_map/ppermute | solution.py:193
  (88 shorter events, 41.1 us)
Async XLA Ops:
  5.9 10.0 %collective-permute-start.3 = (bf16[8,128,128]{2,1,0:T(8,128)(2,1)S(1)}, bf16[8,128,128]{2,1,0:T(8,128)(2,1)S(1)}, u32[]{:S(2)}, u32[]{:S(2)}) collective-permute-start(bf16[8,128,128]{2,1,0:T(8,128)(2,1)S(1)} %get-tuple-element.37), channel_id=1, source_target_pairs={{0,2},{1,3},{2,0},{3,1},{4,6},{5,7},{6,4},{7,5},{8,10},{9,11},{10,... | collective-permute-start | bytes 786440 | tf_op jit(solution)/shard_map/ppermute | solution.py:193
  8.8 12.4 %collective-permute-start.5 = (bf16[8,128,128]{2,1,0:T(8,128)(2,1)S(1)}, bf16[8,128,128]{2,1,0:T(8,128)(2,1)}, u32[]{:S(2)}, u32[]{:S(2)}) collective-permute-start(bf16[8,128,128]{2,1,0:T(8,128)(2,1)S(1)} %get-tuple-element.38), channel_id=1, source_target_pairs={{0,2},{1,3},{2,0},{3,1},{4,6},{5,7},{6,4},{7,5},{8,10},{9,11},{10,... | collective-permute-start | bytes 786440 | tf_op jit(solution)/shard_map/ppermute | solution.py:193
  9.7 24.4 %collective-permute-start.27 = (bf16[1024,256]{1,0:T(8,128)(2,1)}, bf16[1024,256]{1,0:T(8,128)(2,1)}, u32[]{:S(2)}, u32[]{:S(2)}) collective-permute-start(bf16[1024,256]{1,0:T(8,128)(2,1)} %dynamic-slice_bitcast_fusion), channel_id=1, source_target_pairs={{0,1},{1,0},{2,3},{3,2},{4,5},{5,4},{6,7},{7,6},{8,9},{9,8},{10,11... | collective-permute-start | bytes 1572872 | tf_op jit(solution)/shard_map/ppermute | solution.py:193
  21.2 11.5 %collective-permute-start.6 = (bf16[8,128,128]{2,1,0:T(8,128)(2,1)}, bf16[8,128,128]{2,1,0:T(8,128)(2,1)}, u32[]{:S(2)}, u32[]{:S(2)}) collective-permute-start(bf16[8,128,128]{2,1,0:T(8,128)(2,1)} %collective-permute-done.5.refs_2_), channel_id=1, source_target_pairs={{0,1},{1,0},{2,3},{3,2},{4,5},{5,4},{6,7},{7,6},{8,9},{9,8},{10,11... | collective-permute-start | bytes 786440 | tf_op jit(solution)/shard_map/ppermute | solution.py:193
  24.8 12.1 %collective-permute-start.22 = (bf16[2,128,128]{2,1,0:T(8,128)(2,1)S(1)}, bf16[2,128,128]{2,1,0:T(8,128)(2,1)S(1)}, u32[]{:S(2)}, u32[]{:S(2)}) collective-permute-start(bf16[2,128,128]{2,1,0:T(8,128)(2,1)S(1)} %get-tuple-element.47), channel_id=1, source_target_pairs={{0,16},{4,20},{8,24},{12,28},{16,0},{20,4},{24,8},{28,12},{1,17},{... | collective-permute-start | bytes 196616 | tf_op jit(solution)/shard_map/ppermute | solution.py:196
  27.8 11.8 %collective-permute-start.23 = (bf16[2,128,128]{2,1,0:T(8,128)(2,1)S(1)}, bf16[2,128,128]{2,1,0:T(8,128)(2,1)S(1)}, u32[]{:S(2)}, u32[]{:S(2)}) collective-permute-start(bf16[2,128,128]{2,1,0:T(8,128)(2,1)S(1)} %get-tuple-element.48), channel_id=1, source_target_pairs={{0,20},{4,16},{8,28},{12,24},{16,4},{20,0},{24,12},{28,8},{1,21},{... | collective-permute-start | bytes 196616 | tf_op jit(solution)/shard_map/ppermute | solution.py:196
  29.0 15.8 %collective-permute-start.24 = (bf16[2,128,128]{2,1,0:T(8,128)(2,1)S(1)}, bf16[2,128,128]{2,1,0:T(8,128)(2,1)S(1)}, u32[]{:S(2)}, u32[]{:S(2)}) collective-permute-start(bf16[2,128,128]{2,1,0:T(8,128)(2,1)S(1)} %get-tuple-element.49), channel_id=1, source_target_pairs={{0,24},{4,28},{8,16},{12,20},{16,8},{20,12},{24,0},{28,4},{1,25},{... | collective-permute-start | bytes 196616 | tf_op jit(solution)/shard_map/ppermute | solution.py:196
  34.0 10.8 %collective-permute-start.14 = (bf16[2,128,128]{2,1,0:T(8,128)(2,1)S(1)}, bf16[2,128,128]{2,1,0:T(8,128)(2,1)S(1)}, u32[]{:S(2)}, u32[]{:S(2)}) collective-permute-start(bf16[2,128,128]{2,1,0:T(8,128)(2,1)S(1)} %get-tuple-element.43), channel_id=1, source_target_pairs={{0,16},{4,20},{8,24},{12,28},{16,0},{20,4},{24,8},{28,12},{1,17},{... | collective-permute-start | bytes 196616 | tf_op jit(solution)/shard_map/ppermute | solution.py:196
  34.1 13.2 %collective-permute-start.16 = (bf16[2,128,128]{2,1,0:T(8,128)(2,1)S(1)}, bf16[2,128,128]{2,1,0:T(8,128)(2,1)S(1)}, u32[]{:S(2)}, u32[]{:S(2)}) collective-permute-start(bf16[2,128,128]{2,1,0:T(8,128)(2,1)S(1)} %get-tuple-element.44), channel_id=1, source_target_pairs={{0,20},{4,16},{8,28},{12,24},{16,4},{20,0},{24,12},{28,8},{1,21},{... | collective-permute-start | bytes 196616 | tf_op jit(solution)/shard_map/ppermute | solution.py:196
  36.9 11.8 %collective-permute-start.18 = (bf16[2,128,128]{2,1,0:T(8,128)(2,1)S(1)}, bf16[2,128,128]{2,1,0:T(8,128)(2,1)S(1)}, u32[]{:S(2)}, u32[]{:S(2)}) collective-permute-start(bf16[2,128,128]{2,1,0:T(8,128)(2,1)S(1)} %get-tuple-element.45), channel_id=1, source_target_pairs={{0,24},{4,28},{8,16},{12,20},{16,8},{20,12},{24,0},{28,4},{1,25},{... | collective-permute-start | bytes 196616 | tf_op jit(solution)/shard_map/ppermute | solution.py:196
  39.5 9.8 %collective-permute-start.25 = (bf16[2,128,128]{2,1,0:T(8,128)(2,1)S(1)}, bf16[2,128,128]{2,1,0:T(8,128)(2,1)S(1)}, u32[]{:S(2)}, u32[]{:S(2)}) collective-permute-start(bf16[2,128,128]{2,1,0:T(8,128)(2,1)S(1)} %get-tuple-element.50), channel_id=1, source_target_pairs={{0,28},{4,24},{8,20},{12,16},{16,12},{20,8},{24,4},{28,0},{1,29},{... | collective-permute-start | bytes 196616 | tf_op jit(solution)/shard_map/ppermute | solution.py:196
  49.3 15.0 %collective-permute-start.8 = (bf16[2,128,256]{2,1,0:T(8,128)(2,1)S(1)}, bf16[2,128,256]{2,1,0:T(8,128)(2,1)S(1)}, u32[]{:S(2)}, u32[]{:S(2)}) collective-permute-start(bf16[2,128,256]{2,1,0:T(8,128)(2,1)S(1)} %get-tuple-element.40), channel_id=1, source_target_pairs={{0,4},{4,0},{8,12},{12,8},{16,20},{20,16},{24,28},{28,24},{1,5},{5... | collective-permute-start | bytes 393224 | tf_op jit(solution)/shard_map/ppermute | solution.py:196
  51.8 13.1 %collective-permute-start.10 = (bf16[2,128,256]{2,1,0:T(8,128)(2,1)S(1)}, bf16[2,128,256]{2,1,0:T(8,128)(2,1)S(1)}, u32[]{:S(2)}, u32[]{:S(2)}) collective-permute-start(bf16[2,128,256]{2,1,0:T(8,128)(2,1)S(1)} %get-tuple-element.41), channel_id=1, source_target_pairs={{0,8},{4,12},{8,0},{12,4},{16,24},{20,28},{24,16},{28,20},{1,9},{5... | collective-permute-start | bytes 393224 | tf_op jit(solution)/shard_map/ppermute | solution.py:196
  53.4 12.9 %collective-permute-start.12 = (bf16[2,128,256]{2,1,0:T(8,128)(2,1)S(1)}, bf16[2,128,256]{2,1,0:T(8,128)(2,1)S(1)}, u32[]{:S(2)}, u32[]{:S(2)}) collective-permute-start(bf16[2,128,256]{2,1,0:T(8,128)(2,1)S(1)} %get-tuple-element.42), channel_id=1, source_target_pairs={{0,12},{4,8},{8,4},{12,0},{16,28},{20,24},{24,20},{28,16},{1,13},{... | collective-permute-start | bytes 393224 | tf_op jit(solution)/shard_map/ppermute | solution.py:196
  53.7 21.6 %collective-permute-start.26 = (bf16[4,2,128,128]{3,2,1,0:T(8,128)(2,1)S(1)}, bf16[4,2,128,128]{3,2,1,0:T(8,128)(2,1)S(1)}, u32[]{:S(2)}, u32[]{:S(2)}) collective-permute-start(bf16[4,2,128,128]{3,2,1,0:T(8,128)(2,1)S(1)} %shard_map.90), channel_id=1, source_target_pairs={{0,2},{1,3},{2,0},{3,1},{4,6},{5,7},{6,4},{7,5},{8,10},{9,11},{10,... | collective-permute-start | bytes 786440 | tf_op jit(solution)/shard_map/ppermute | solution.py:193
  78.0 38.3 %collective-permute-start.28 = (bf16[1024,1024]{1,0:T(8,128)(2,1)S(1)}, bf16[1024,1024]{1,0:T(8,128)(2,1)S(1)}, u32[]{:S(2)}, u32[]{:S(2)}) collective-permute-start(bf16[1024,1024]{1,0:T(8,128)(2,1)S(1)} %get-tuple-element.53.grad_ref), channel_id=1, source_target_pairs={{0,1},{1,0},{2,3},{3,2},{4,5},{5,4},{6,7},{7,6},{8,9},{9,8},{10,11... | collective-permute-start | bytes 6291464 | tf_op jit(solution)/shard_map/ppermute | solution.py:193
  85.1 13.3 %collective-permute-start.33 = (bf16[2,256,256]{2,1,0:T(8,128)(2,1)S(1)}, bf16[2,256,256]{2,1,0:T(8,128)(2,1)S(1)}, u32[]{:S(2)}, u32[]{:S(2)}) collective-permute-start(bf16[2,256,256]{2,1,0:T(8,128)(2,1)S(1)} %get-tuple-element.63.near_ref), channel_id=1, source_target_pairs={{0,2},{1,3},{2,0},{3,1},{4,6},{5,7},{6,4},{7,5},{8,10},{9,11},{10,... | collective-permute-start | bytes 786440 | tf_op jit(solution)/shard_map/ppermute | solution.py:193
  85.7 18.4 %collective-permute-start.30 = (bf16[2,256,256]{2,1,0:T(8,128)(2,1)S(1)}, bf16[2,256,256]{2,1,0:T(8,128)(2,1)S(1)}, u32[]{:S(2)}, u32[]{:S(2)}) collective-permute-start(bf16[2,256,256]{2,1,0:T(8,128)(2,1)S(1)} %get-tuple-element.60.near_ref), channel_id=1, source_target_pairs={{0,2},{1,3},{2,0},{3,1},{4,6},{5,7},{6,4},{7,5},{8,10},{9,11},{10,... | collective-permute-start | bytes 786440 | tf_op jit(solution)/shard_map/ppermute | solution.py:193
  87.2 21.7 %collective-permute-start.1 = (bf16[2,256,256]{2,1,0:T(8,128)(2,1)S(1)}, bf16[2,256,256]{2,1,0:T(8,128)(2,1)S(1)}, u32[]{:S(2)}, u32[]{:S(2)}) collective-permute-start(bf16[2,256,256]{2,1,0:T(8,128)(2,1)S(1)} %get-tuple-element.36.near_ref), channel_id=1, source_target_pairs={{0,2},{1,3},{2,0},{3,1},{4,6},{5,7},{6,4},{7,5},{8,10},{9,11},{10,... | collective-permute-start | bytes 786440 | tf_op jit(solution)/shard_map/ppermute | solution.py:193
  93.8 20.5 %collective-permute-start.37 = (bf16[2,128,256]{2,1,0:T(8,128)(2,1)S(1)}, bf16[2,128,256]{2,1,0:T(8,128)(2,1)S(1)}, u32[]{:S(2)}, u32[]{:S(2)}) collective-permute-start(bf16[2,128,256]{2,1,0:T(8,128)(2,1)S(1)} %get-tuple-element.67), channel_id=1, source_target_pairs={{0,24},{4,28},{8,16},{12,20},{16,8},{20,12},{24,0},{28,4},{1,25},{... | collective-permute-start | bytes 393224 | tf_op jit(solution)/shard_map/ppermute | solution.py:196
  98.4 16.6 %collective-permute-start.38 = (bf16[2,128,256]{2,1,0:T(8,128)(2,1)S(1)}, bf16[2,128,256]{2,1,0:T(8,128)(2,1)S(1)}, u32[]{:S(2)}, u32[]{:S(2)}) collective-permute-start(bf16[2,128,256]{2,1,0:T(8,128)(2,1)S(1)} %get-tuple-element.68), channel_id=1, source_target_pairs={{0,28},{4,24},{8,20},{12,16},{16,12},{20,8},{24,4},{28,0},{1,29},{... | collective-permute-start | bytes 393224 | tf_op jit(solution)/shard_map/ppermute | solution.py:196
  104.0 18.6 %collective-permute-start.34 = (bf16[2,128,256]{2,1,0:T(8,128)(2,1)S(1)}, bf16[2,128,256]{2,1,0:T(8,128)(2,1)S(1)}, u32[]{:S(2)}, u32[]{:S(2)}) collective-permute-start(bf16[2,128,256]{2,1,0:T(8,128)(2,1)S(1)} %get-tuple-element.64), channel_id=1, source_target_pairs={{0,16},{4,20},{8,24},{12,28},{16,0},{20,4},{24,8},{28,12},{1,17},{... | collective-permute-start | bytes 393224 | tf_op jit(solution)/shard_map/ppermute | solution.py:196
  108.8 13.8 %collective-permute-start.35 = (bf16[2,128,256]{2,1,0:T(8,128)(2,1)S(1)}, bf16[2,128,256]{2,1,0:T(8,128)(2,1)S(1)}, u32[]{:S(2)}, u32[]{:S(2)}) collective-permute-start(bf16[2,128,256]{2,1,0:T(8,128)(2,1)S(1)} %get-tuple-element.65), channel_id=1, source_target_pairs={{0,20},{4,16},{8,28},{12,24},{16,4},{20,0},{24,12},{28,8},{1,21},{... | collective-permute-start | bytes 393224 | tf_op jit(solution)/shard_map/ppermute | solution.py:196
  115.1 10.2 %collective-permute-start.32 = (bf16[2,128,256]{2,1,0:T(8,128)(2,1)S(1)}, bf16[2,128,256]{2,1,0:T(8,128)(2,1)S(1)}, u32[]{:S(2)}, u32[]{:S(2)}) collective-permute-start(bf16[2,128,256]{2,1,0:T(8,128)(2,1)S(1)} %get-tuple-element.62), channel_id=1, source_target_pairs={{0,12},{4,8},{8,4},{12,0},{16,28},{20,24},{24,20},{28,16},{1,13},{... | collective-permute-start | bytes 393224 | tf_op jit(solution)/shard_map/ppermute | solution.py:196
  (22 other events, 206.2 us)
where the time goes:
time: 130 us; the launch traced here: 129 us
  starting transfers between devices  56.2 us (43%)
  waiting for transfers between devices  50.6 us (39%)
  Pallas kernels  18 us (14%)
  local copies, waits for them, and re-layouts  3.72 us (3%)
    ppermute x22, waiting for transfers between devices, swap(): return lax.ppermute(x, 'rep', [(r, r ^ bits) for r in range(quarters)])  42.6 us
    ppermute x18, starting transfers between devices, give(): return lax.ppermute(x, 'fsdp', [(f, f ^ k) for f in range(owners)])  38.2 us
    ppermute x22, starting transfers between devices, swap(): return lax.ppermute(x, 'rep', [(r, r ^ bits) for r in range(quarters)])  18 us
    pallas_call x13, Pallas kernels, call(): pl.pallas_call(kernel, out_shape=out_shape, in_specs=[smem] * len(scalars...  13.3 us
    ppermute x18, waiting for transfers between devices, give(): return lax.ppermute(x, 'fsdp', [(f, f ^ k) for f in range(owners)])  8.01 us
    pallas_call x1, Pallas kernels, stats(): pl.pallas_call(stats_kernel, grid_spec=pltpu.PrefetchScalarGridSpec(num_s...  4.69 us
  transfers between devices with their start and end apart: 40, of which 18 were waited for; matrix products, arithmetic and copies ran while one was open for 2% of the time, Pallas kernels for 10%

commit v1 on v0

--- a/solution.py
+++ b/solution.py
@@ -11,19 +11,18 @@
 decay_rate = 0.99
 
 
-def pair_kernel(where_ref, mine_ref, near_ref, *outs):
-    width = mine_ref.shape[2]
-    cols = pl.ds(pl.multiple_of((where_ref[1] ^ 2) * width, width), width)
-    total = (mine_ref[...].astype(jnp.float32) + near_ref[:, :, cols].astype(jnp.float32)).astype(jnp.bfloat16)
-    for p in range(2):
-        outs[p][...] = total[:, :, p * width // 2 : (p + 1) * width // 2]
-
-
-def base_kernel(where_ref, grad_ref, near_ref, out_ref):
-    width = out_ref.shape[3]
+def first_pair_kernel(mine_ref, near_ref, out_ref):
+    out_ref[...] = (mine_ref[...].astype(jnp.float32) + near_ref[...].astype(jnp.float32)).astype(jnp.bfloat16)
+
+
+def second_pair_kernel(where_ref, grad_ref, near_ref, out_ref, base_ref):
+    step = out_ref.shape[2]
+    cols = pl.ds(pl.multiple_of((where_ref[1] ^ 2) * 2 * step + step, step), step)
+    total = grad_ref[:, :, cols].astype(jnp.float32) + near_ref[:, :, cols].astype(jnp.float32)
+    out_ref[...] = total.astype(jnp.bfloat16)
     for q in range(2):
-        cols = pl.ds(pl.multiple_of((where_ref[1] ^ q) * width, width), width)
-        out_ref[q] = grad_ref[:, :, cols].astype(jnp.float32) + near_ref[:, :, cols].astype(jnp.float32)
+        cols = pl.ds(pl.multiple_of((where_ref[1] ^ q) * 2 * step, 2 * step), 2 * step)
+        base_ref[q] = grad_ref[:, :, cols].astype(jnp.float32) + near_ref[:, :, cols].astype(jnp.float32)
 
 
 def route_kernel(wanted, table_ref, where_ref, base_ref, *refs):
@@ -31,7 +30,7 @@
     me, side = where_ref[0], where_ref[1] & 1
     step = sums[0].shape[2]
     for (k, parts), piece in zip(wanted, pieces):
-        block = table_ref[(me ^ k) * 2 + side]
+        block = table_ref[side, me ^ k]
 
         @pl.when(block >= 0)
         def _(parts=parts, piece=piece, block=block):
@@ -91,11 +90,16 @@
         odd_ref[side ^ i] = jnp.where(swapped, total[:rows], total[rows:])
 
 
+def product_apply_kernel(owners, where_ref, near_ref, far_ref, *refs):
+    product_kernel(owners, where_ref, *refs[:-2])
+    apply_kernel(where_ref, near_ref, far_ref, *refs[-3:])
+
+
 def stats_kernel(table_ref, where_ref, grad_ref, other_ref, left_ref, right_ref, left_out, right_out):
     me, rep = where_ref[0], where_ref[1]
     _, _, width = left_ref.shape
     slot = pl.program_id(0)
-    filled = table_ref[me * 2 + slot] >= 0
+    filled = table_ref[slot, me] >= 0
     share = pl.ds(pl.multiple_of(rep * width, width), width)
 
     def update(ref):
@@ -135,37 +139,41 @@
     )(table, where, grad, other, left, right)
 
 
-def left_kernel(both, where_ref, left_ref, near_ref, *parts):
+def left_kernel(pairs, where_ref, left_ref, near_ref, *parts):
+    both = parts[0].shape[1]
     me, side = where_ref[0], where_ref[1] & 1
-    for j in range(len(parts)):
+    for j, part in zip(pairs, parts):
         rows = pl.ds(pl.multiple_of(((me >> 1) ^ j) * both, both), both)
-        parts[j][0] = left_ref[side, rows, :]
-        parts[j][1] = near_ref[rows, :]
-
-
-def pack_kernel(owners, where_ref, *refs):
-    for k in range(owners):
-        refs[-1][k] = refs[k][1 - (where_ref[1] & 1)]
-
-
-def collect_kernel(owners, table_ref, where_ref, *refs):
-    pieces, beside_ref, out_ref = refs[:-2], refs[-2], refs[-1]
+        part[0] = left_ref[side, rows, :]
+        part[1] = near_ref[rows, :]
+
+
+def pack_kernel(where_ref, *refs):
+    for n in range(len(refs) - 1):
+        refs[-1][n] = refs[n][1 - (where_ref[1] & 1)]
+
+
+def collect_kernel(owners, packed, late, table_ref, where_ref, *refs):
+    pieces, out_ref = refs[:owners], refs[-1]
     me, side = where_ref[0], where_ref[1] & 1
     for k in range(owners):
-        block = table_ref[(me ^ k) * 2 + side]
+        block = table_ref[side, me ^ k]
 
         @pl.when(block >= 0)
         def _(k=k, block=block):
             out_ref[block] = pieces[k][side]
 
-        beside = table_ref[(me ^ k) * 2 + 1 - side]
-
-        @pl.when(beside >= 0)
-        def _(k=k, beside=beside):
-            out_ref[beside] = beside_ref[k]
-
-
-def call(kernel, scalars, out_shape, ins, scratch=()):
+        other = table_ref[1 - side, me ^ k]
+
+        @pl.when(other >= 0)
+        def _(k=k, other=other):
+            if k in late:
+                out_ref[other] = refs[owners + 1 + late.index(k)][side]
+            else:
+                out_ref[other] = refs[owners][packed.index(k)]
+
+
+def call(kernel, scalars, out_shape, ins, limit=8):
     vmem = pl.BlockSpec(memory_space=pltpu.VMEM)
     smem = pl.BlockSpec(memory_space=pltpu.SMEM)
     return pl.pallas_call(
@@ -173,8 +181,7 @@
         out_shape=out_shape,
         in_specs=[smem] * len(scalars) + [vmem] * len(ins),
         out_specs=jax.tree.map(lambda _: vmem, out_shape),
-        scratch_shapes=scratch,
-        compiler_params=pltpu.CompilerParams(vmem_limit_bytes=24 * 1024 * 1024),
+        compiler_params=pltpu.CompilerParams(vmem_limit_bytes=limit * 1024 * 1024),
     )(*scalars, *ins)
 
 
@@ -185,7 +192,7 @@
     slots, order, width = left_stat.shape[1:]
     assert slots == 2
     rows = grad.shape[1]
-    table = owner_table.reshape(-1)
+    table = owner_table.T
     where = jnp.stack([me, rep]).astype(jnp.int32)
     bf16 = lambda *shape: jax.ShapeDtypeStruct(shape, jnp.bfloat16)
 
@@ -198,23 +205,30 @@
     def slot(x, s):
         return lax.dynamic_index_in_dim(x, s, 0, keepdims=False)
 
+    def cut(q):
+        return lax.dynamic_slice_in_dim(grad, q * width, width // 2, 2)
+
+    half = bf16(grad.shape[0], rows, width // 2)
+    lead = swap(cut(rep ^ 3), 1)
     near = swap(grad, 1)
-    part = lax.dynamic_slice_in_dim(grad, (rep ^ 2) * width, width, 2)
-    halves = call(pair_kernel, (where,), (bf16(grad.shape[0], rows, width // 2),) * 2, (part, near))
-    across = [swap(halves[p], 2) for p in range(2)]
-    base = jax.ShapeDtypeStruct((2, *part.shape), jnp.float32)
-    base = call(base_kernel, (where,), base, (grad, near))
+    first = call(first_pair_kernel, (), half, (cut(rep ^ 2), lead))
+    base = jax.ShapeDtypeStruct((2, grad.shape[0], rows, width), jnp.float32)
+    second, base = call(second_pair_kernel, (where,), (half, base), (grad, near))
+    across = [swap(first, 2), swap(second, 2)]
     beside = [swap(across[p], 1) for p in range(2)]
     left, right = left_root[0], right_root[0]
     left_near = swap(slot(left, 1 - side), 1)
     right_near = swap(slot(right, 1 - side), 1)
-    left_parts = call(
-        functools.partial(left_kernel, 2 * rows),
-        (where,),
-        (bf16(2, 2 * rows, width),) * (owners // 2),
-        (left, left_near),
-    )
     half = owners // 2
+    left_parts = {}
+    for pairs in ([half - 1, half - 2], list(range(half - 2))):
+        parts = call(
+            functools.partial(left_kernel, pairs),
+            (where,),
+            (bf16(2, 2 * rows, width),) * len(pairs),
+            (left, left_near),
+        )
+        left_parts.update(zip(pairs, parts))
     piece, split = bf16(2, rows, width), bf16(2, rows, width // 2)
     early = call(
         functools.partial(route_kernel, [(k, (0,)) for k in range(half, owners)]),
@@ -235,29 +249,34 @@
     for k in range(owners):
         own = give(pieces[k], k) if k else pieces[k]
         gathered += [own, swap(own, 2)]
-    gradient, product = call(
-        functools.partial(product_kernel, owners),
-        (where,),
-        (bf16(order, order), bf16(2, order, width)),
-        (*gathered, *early, joined, right, right_near),
-    )
     returned = {}
-    for j in reversed(range(owners // 2)):
+    result = bf16(2, rows, width)
+    for j in reversed(range(half)):
         part = left_parts[j]
         far = swap(part, 2)
-        same, odd = call(apply_kernel, (where,), (bf16(2, rows, width),) * 2, (part, far, product))
+        if j == half - 1:
+            gradient, product, same, odd = call(
+                functools.partial(product_apply_kernel, owners),
+                (where,),
+                (bf16(order, order), bf16(2, order, width), result, result),
+                (part, far, *gathered, *early, joined, right, right_near),
+                12,
+            )
+        else:
+            same, odd = call(apply_kernel, (where,), (result, result), (part, far, product))
         returned[2 * j + 1] = give(odd, 2 * j + 1)
         returned[2 * j] = give(same, 2 * j) if j else same
     other = swap(gradient, 1)
     left_next, right_next = stats(table, where, gradient, other, left_stat[0], right_stat[0])
-    returned[0], left_next, right_next = lax.optimization_barrier((returned[0], left_next, right_next))
-    returned = [returned[k] for k in range(owners)]
-    packed = call(functools.partial(pack_kernel, owners), (where,), bf16(owners, rows, width), returned)
+    late = [2, 3, half]
+    packed = [k for k in range(owners) if k not in late]
+    beside = [call(pack_kernel, (where,), bf16(len(packed), rows, width), [returned[k] for k in packed])]
+    beside = [swap(beside[0], 1)] + [swap(returned[k], 1) for k in late]
     update = call(
-        functools.partial(collect_kernel, owners),
+        functools.partial(collect_kernel, owners, packed, late),
         (table, where),
         bf16(grad.shape[0], rows, width),
-        (*returned, swap(packed, 1)),
+        (*(returned[k] for k in range(owners)), *beside),
     )
     return left_next[None], right_next[None], update
 

time: 130 us -> 123 us (0.946)
  starting transfers between devices: 56.2 us -> 49.2 us
    ppermute x18, waiting for transfers between devices: 8.01 us -> 16 us  [give(): return lax.ppermute(x, 'fsdp', [(f, f ^ k) for f in range(owners)])]
    ppermute x22 -> x26, waiting for transfers between devices: 42.6 us -> 34.9 us  [swap(): return lax.ppermute(x, 'rep', [(r, r ^ bits) for r in range(quarters)])]
    ppermute x18, starting transfers between devices: 38.2 us -> 31.5 us  [give(): return lax.ppermute(x, 'fsdp', [(f, f ^ k) for f in range(owners)])]
    ppermute x22 -> x26, starting transfers between devices: 18 us -> 17.7 us  [swap(): return lax.ppermute(x, 'rep', [(r, r ^ bits) for r in range(quarters)])]
  transfers between devices with their start and end apart: 40 -> 44, of which waited for: 18 -> 17; matrix products, arithmetic and copies ran while one was open for 2% -> 2% of each run, Pallas kernels for 10% -> 9%
where the time goes in v1:
time: 123 us; the launch traced here: 122 us
  waiting for transfers between devices  50.9 us (41%)
  starting transfers between devices  49.2 us (40%)
  Pallas kernels  17.7 us (14%)
  local copies, waits for them, and re-layouts  3.55 us (3%)
    ppermute x26, waiting for transfers between devices, swap(): return lax.ppermute(x, 'rep', [(r, r ^ bits) for r in range(quarters)])  34.9 us
    ppermute x18, starting transfers between devices, give(): return lax.ppermute(x, 'fsdp', [(f, f ^ k) for f in range(owners)])  31.5 us
    ppermute x26, starting transfers between devices, swap(): return lax.ppermute(x, 'rep', [(r, r ^ bits) for r in range(quarters)])  17.7 us
    ppermute x18, waiting for transfers between devices, give(): return lax.ppermute(x, 'fsdp', [(f, f ^ k) for f in range(owners)])  16 us
    pallas_call x13, Pallas kernels, call(): pl.pallas_call(kernel, out_shape=out_shape, in_specs=[smem] * len(scalars...  13.1 us
    pallas_call x1, Pallas kernels, stats(): pl.pallas_call(stats_kernel, grid_spec=pltpu.PrefetchScalarGridSpec(num_s...  4.69 us
  transfers between devices with their start and end apart: 44, of which 17 were waited for; matrix products, arithmetic and copies ran while one was open for 2% of the time, Pallas kernels for 9%

profile of v1, /device:TPU:0, one launch (start us, length us, event | category | flops | bytes accessed | tf_op | source)
XLA Modules:
  0.0 122.3 jit_solution(2256320074064662735)
XLA Ops:
  2.4 3.1 %collective-permute-done.3.near_ref = bf16[8,128,128]{2,1,0:T(8,128)(2,1)S(1)} collective-permute-done((bf16[8,128,128]{2,1,0:T(8,128)(2,1)S(1)}, bf16[8,128,128]{2,1,0:T(8,128)(2,1)S(1)}, u32[]{:S(2)}, u32[]{:S(2)}) %collective-permute-start.3) | collective-permute-done | bytes 262176 | tf_op jit(solution)/shard_map/ppermute | solution.py:200
  6.3 2.8 %collective-permute-start.4 = (bf16[8,128,128]{2,1,0:T(8,128)(2,1)}, bf16[8,128,128]{2,1,0:T(8,128)(2,1)S(1)}, u32[]{:S(2)}, u32[]{:S(2)}) collective-permute-start(bf16[8,128,128]{2,1,0:T(8,128)(2,1)} %shard_map.87), channel_id=1, source_target_pairs={{0,2},{1,3},{2,0},{3,1},{4,6},{5,7},{6,4},{7,5},{8,10},{9,11},{10,... | collective-permute-start | bytes 786440 | tf_op jit(solution)/shard_map/ppermute | solution.py:200
  10.0 6.0 %collective-permute-done.4.refs_0_ = bf16[8,128,128]{2,1,0:T(8,128)(2,1)S(1)} collective-permute-done((bf16[8,128,128]{2,1,0:T(8,128)(2,1)}, bf16[8,128,128]{2,1,0:T(8,128)(2,1)S(1)}, u32[]{:S(2)}, u32[]{:S(2)}) %collective-permute-start.4) | collective-permute-done | bytes 262176 | tf_op jit(solution)/shard_map/ppermute | solution.py:200
  21.4 2.7 %collective-permute-start.23 = (bf16[2,128,128]{2,1,0:T(8,128)(2,1)S(1)}, bf16[2,128,128]{2,1,0:T(8,128)(2,1)S(1)}, u32[]{:S(2)}, u32[]{:S(2)}) collective-permute-start(bf16[2,128,128]{2,1,0:T(8,128)(2,1)S(1)} %get-tuple-element.44), channel_id=1, source_target_pairs={{0,16},{4,20},{8,24},{12,28},{16,0},{20,4},{24,8},{28,12},{1,17},{... | collective-permute-start | bytes 196616 | tf_op jit(solution)/shard_map/ppermute | solution.py:203
  25.4 3.6 %collective-permute-start.25 = (bf16[2,128,128]{2,1,0:T(8,128)(2,1)S(1)}, bf16[2,128,128]{2,1,0:T(8,128)(2,1)S(1)}, u32[]{:S(2)}, u32[]{:S(2)}) collective-permute-start(bf16[2,128,128]{2,1,0:T(8,128)(2,1)S(1)} %get-tuple-element.46), channel_id=1, source_target_pairs={{0,24},{4,28},{8,16},{12,20},{16,8},{20,12},{24,0},{28,4},{1,25},{... | collective-permute-start | bytes 196616 | tf_op jit(solution)/shard_map/ppermute | solution.py:203
  29.0 6.4 %collective-permute-start.26 = (bf16[2,128,128]{2,1,0:T(8,128)(2,1)S(1)}, bf16[2,128,128]{2,1,0:T(8,128)(2,1)S(1)}, u32[]{:S(2)}, u32[]{:S(2)}) collective-permute-start(bf16[2,128,128]{2,1,0:T(8,128)(2,1)S(1)} %get-tuple-element.47), channel_id=1, source_target_pairs={{0,28},{4,24},{8,20},{12,16},{16,12},{20,8},{24,4},{28,0},{1,29},{... | collective-permute-start | bytes 196616 | tf_op jit(solution)/shard_map/ppermute | solution.py:203
  39.5 2.0 %collective-permute-start.15 = (bf16[2,128,128]{2,1,0:T(8,128)(2,1)S(1)}, bf16[2,128,128]{2,1,0:T(8,128)(2,1)S(1)}, u32[]{:S(2)}, u32[]{:S(2)}) collective-permute-start(bf16[2,128,128]{2,1,0:T(8,128)(2,1)S(1)} %get-tuple-element.40), channel_id=1, source_target_pairs={{0,16},{4,20},{8,24},{12,28},{16,0},{20,4},{24,8},{28,12},{1,17},{... | collective-permute-start | bytes 196616 | tf_op jit(solution)/shard_map/ppermute | solution.py:203
  41.6 5.2 %collective-permute-start.19 = (bf16[2,128,128]{2,1,0:T(8,128)(2,1)S(1)}, bf16[2,128,128]{2,1,0:T(8,128)(2,1)S(1)}, u32[]{:S(2)}, u32[]{:S(2)}) collective-permute-start(bf16[2,128,128]{2,1,0:T(8,128)(2,1)S(1)} %get-tuple-element.42), channel_id=1, source_target_pairs={{0,24},{4,28},{8,16},{12,20},{16,8},{20,12},{24,0},{28,4},{1,25},{... | collective-permute-start | bytes 196616 | tf_op jit(solution)/shard_map/ppermute | solution.py:203
  47.2 3.7 %collective-permute-done.27.refs_20_ = bf16[4,2,128,128]{3,2,1,0:T(8,128)(2,1)S(1)} collective-permute-done((bf16[4,2,128,128]{3,2,1,0:T(8,128)(2,1)S(1)}, bf16[4,2,128,128]{3,2,1,0:T(8,128)(2,1)S(1)}, u32[]{:S(2)}, u32[]{:S(2)}) %collective-permute-start.27) | collective-permute-done | bytes 262176 | tf_op jit(solution)/shard_map/ppermute | solution.py:200
  51.1 3.3 %collective-permute-start.13 = (bf16[2,128,256]{2,1,0:T(8,128)(2,1)S(1)}, bf16[2,128,256]{2,1,0:T(8,128)(2,1)S(1)}, u32[]{:S(2)}, u32[]{:S(2)}) collective-permute-start(bf16[2,128,256]{2,1,0:T(8,128)(2,1)S(1)} %get-tuple-element.39), channel_id=1, source_target_pairs={{0,12},{4,8},{8,4},{12,0},{16,28},{20,24},{24,20},{28,16},{1,13},{... | collective-permute-start | bytes 393224 | tf_op jit(solution)/shard_map/ppermute | solution.py:203
  56.5 2.2 %collective-permute-done.16.refs_9_ = bf16[2,128,128]{2,1,0:T(8,128)(2,1)S(1)} collective-permute-done((bf16[2,128,128]{2,1,0:T(8,128)(2,1)S(1)}, bf16[2,128,128]{2,1,0:T(8,128)(2,1)S(1)}, u32[]{:S(2)}, u32[]{:S(2)}) %collective-permute-start.16) | collective-permute-done | bytes 65568 | tf_op jit(solution)/shard_map/ppermute | solution.py:200
  59.5 1.9 %collective-permute-start.20 = (bf16[2,128,128]{2,1,0:T(8,128)(2,1)S(1)}, bf16[2,128,128]{2,1,0:T(8,128)(2,1)S(1)}, u32[]{:S(2)}, u32[]{:S(2)}) collective-permute-start(bf16[2,128,128]{2,1,0:T(8,128)(2,1)S(1)} %collective-permute-done.19.refs_12_), channel_id=1, source_target_pairs={{0,2},{1,3},{2,0},{3,1},{4,6},{5,7},{6,4},{7,5},{8,10},{9,11},{10,... | collective-permute-start | bytes 196616 | tf_op jit(solution)/shard_map/ppermute | solution.py:200
  61.6 1.9 %collective-permute-start.12 = (bf16[2,128,256]{2,1,0:T(8,128)(2,1)S(1)}, bf16[2,128,256]{2,1,0:T(8,128)(2,1)S(1)}, u32[]{:S(2)}, u32[]{:S(2)}) collective-permute-start(bf16[2,128,256]{2,1,0:T(8,128)(2,1)S(1)} %collective-permute-done.11.refs_4_), channel_id=1, source_target_pairs={{0,2},{1,3},{2,0},{3,1},{4,6},{5,7},{6,4},{7,5},{8,10},{9,11},{10,... | collective-permute-start | bytes 393224 | tf_op jit(solution)/shard_map/ppermute | solution.py:200
  63.6 2.9 %collective-permute-done.20.refs_13_ = bf16[2,128,128]{2,1,0:T(8,128)(2,1)S(1)} collective-permute-done((bf16[2,128,128]{2,1,0:T(8,128)(2,1)S(1)}, bf16[2,128,128]{2,1,0:T(8,128)(2,1)S(1)}, u32[]{:S(2)}, u32[]{:S(2)}) %collective-permute-start.20) | collective-permute-done | bytes 65568 | tf_op jit(solution)/shard_map/ppermute | solution.py:200
  67.0 6.4 %collective-permute-done.22.refs_15_ = bf16[2,128,128]{2,1,0:T(8,128)(2,1)S(1)} collective-permute-done((bf16[2,128,128]{2,1,0:T(8,128)(2,1)S(1)}, bf16[2,128,128]{2,1,0:T(8,128)(2,1)S(1)}, u32[]{:S(2)}, u32[]{:S(2)}) %collective-permute-start.22) | collective-permute-done | bytes 65568 | tf_op jit(solution)/shard_map/ppermute | solution.py:200
  73.5 2.6 %shard_map.91 = (bf16[1024,1024]{1,0:T(8,128)(2,1)S(1)}, bf16[2,1024,256]{2,1,0:T(8,128)(2,1)S(1)}, bf16[2,128,256]{2,1,0:T(8,128)(2,1)S(1)}, bf16[2,128,256]{2,1,0:T(8,128)(2,1)S(1)}) custom-call(s32[2]{0:T(128)S(1)} %pad_add_fusion.where_ref, bf16[2,256,256]{2,1,0:T(8,128)(2,1)S(1)} %get-tuple-element.33.near_ref, ...), custom_call_target="tpu_custom_call" | custom-call | tf_op jit(solution)/shard_map/pallas_call | solution.py:179
  80.5 4.9 %collective-permute-done.35.far_ref = bf16[2,256,256]{2,1,0:T(8,128)(2,1)S(1)} collective-permute-done((bf16[2,256,256]{2,1,0:T(8,128)(2,1)S(1)}, bf16[2,256,256]{2,1,0:T(8,128)(2,1)S(1)}, u32[]{:S(2)}, u32[]{:S(2)}) %collective-permute-start.35) | collective-permute-done | bytes 262176 | tf_op jit(solution)/shard_map/ppermute | solution.py:200
  87.1 4.0 %collective-permute-done.30.far_ref = bf16[2,256,256]{2,1,0:T(8,128)(2,1)S(1)} collective-permute-done((bf16[2,256,256]{2,1,0:T(8,128)(2,1)S(1)}, bf16[2,256,256]{2,1,0:T(8,128)(2,1)S(1)}, u32[]{:S(2)}, u32[]{:S(2)}) %collective-permute-start.30) | collective-permute-done | bytes 262176 | tf_op jit(solution)/shard_map/ppermute | solution.py:200
  94.8 4.9 %collective-permute-done.37.refs_2_.refs_5_ = bf16[2,128,256]{2,1,0:T(8,128)(2,1)S(1)} collective-permute-done((bf16[2,128,256]{2,1,0:T(8,128)(2,1)S(1)}, bf16[2,128,256]{2,1,0:T(8,128)(2,1)S(1)}, u32[]{:S(2)}, u32[]{:S(2)}) %collective-permute-start.37) | collective-permute-done | bytes 131104 | tf_op jit(solution)/shard_map/ppermute | solution.py:203
  103.5 2.1 %collective-permute-start.34 = (bf16[2,128,256]{2,1,0:T(8,128)(2,1)S(1)}, bf16[2,128,256]{2,1,0:T(8,128)(2,1)S(1)}, u32[]{:S(2)}, u32[]{:S(2)}) collective-permute-start(bf16[2,128,256]{2,1,0:T(8,128)(2,1)S(1)} %get-tuple-element.57), channel_id=1, source_target_pairs={{0,12},{4,8},{8,4},{12,0},{16,28},{20,24},{24,20},{28,16},{1,13},{... | collective-permute-start | bytes 393224 | tf_op jit(solution)/shard_map/ppermute | solution.py:203
  105.6 4.3 %collective-permute-done.36.refs_4_ = bf16[2,128,256]{2,1,0:T(8,128)(2,1)S(1)} collective-permute-done((bf16[2,128,256]{2,1,0:T(8,128)(2,1)S(1)}, bf16[2,128,256]{2,1,0:T(8,128)(2,1)S(1)}, u32[]{:S(2)}, u32[]{:S(2)}) %collective-permute-start.36) | collective-permute-done | bytes 131104 | tf_op jit(solution)/shard_map/ppermute | solution.py:203
  110.0 2.3 %collective-permute-done.33.refs_2_ = bf16[2,128,256]{2,1,0:T(8,128)(2,1)S(1)} collective-permute-done((bf16[2,128,256]{2,1,0:T(8,128)(2,1)S(1)}, bf16[2,128,256]{2,1,0:T(8,128)(2,1)S(1)}, u32[]{:S(2)}, u32[]{:S(2)}) %collective-permute-start.33) | collective-permute-done | bytes 131104 | tf_op jit(solution)/shard_map/ppermute | solution.py:203
  112.3 2.5 %collective-permute-done.34.refs_3_ = bf16[2,128,256]{2,1,0:T(8,128)(2,1)S(1)} collective-permute-done((bf16[2,128,256]{2,1,0:T(8,128)(2,1)S(1)}, bf16[2,128,256]{2,1,0:T(8,128)(2,1)S(1)}, u32[]{:S(2)}, u32[]{:S(2)}) %collective-permute-start.34) | collective-permute-done | bytes 131104 | tf_op jit(solution)/shard_map/ppermute | solution.py:203
  117.6 4.7 %shard_map.92 = (f32[2,1024,256]{2,1,0:T(8,128)}, f32[2,1024,256]{2,1,0:T(8,128)}) custom-call(s32[2,8]{1,0:T(2,128)S(1)} %bitcast.28, s32[2]{0:T(128)S(1)} %pad_add_fusion.where_ref, bf16[1024,1024]{1,0:T(8,128)(2,1)S(1)} %get-tuple-element.48.grad_ref, bf16[1024,1024]{1,0:T(8,128)(2,1)S(1)} %collective-permute-done.29.other_ref, ...), custom_call_target="tpu_custom_call" | custom-call | tf_op jit(solution)/shard_map/pallas_call | solution.py:129
  (94 shorter events, 35.0 us)
Async XLA Ops:
  0.6 15.4 %collective-permute-start.2 = (bf16[8,128,1024]{2,1,0:T(8,128)(2,1)}, bf16[8,128,1024]{2,1,0:T(8,128)(2,1)S(1)}, u32[]{:S(2)}, u32[]{:S(2)}) collective-permute-start(bf16[8,128,1024]{2,1,0:T(8,128)(2,1)} %bitcast.20), channel_id=1, source_target_pairs={{0,1},{1,0},{2,3},{3,2},{4,5},{5,4},{6,7},{7,6},{8,9},{9,8},{10,11... | collective-permute-start | bytes 6291464 | tf_op jit(solution)/shard_map/ppermute | solution.py:200
  6.3 9.7 %collective-permute-start.4 = (bf16[8,128,128]{2,1,0:T(8,128)(2,1)}, bf16[8,128,128]{2,1,0:T(8,128)(2,1)S(1)}, u32[]{:S(2)}, u32[]{:S(2)}) collective-permute-start(bf16[8,128,128]{2,1,0:T(8,128)(2,1)} %shard_map.87), channel_id=1, source_target_pairs={{0,2},{1,3},{2,0},{3,1},{4,6},{5,7},{6,4},{7,5},{8,10},{9,11},{10,... | collective-permute-start | bytes 786440 | tf_op jit(solution)/shard_map/ppermute | solution.py:200
  10.0 15.4 %collective-permute-start = (bf16[1024,256]{1,0:T(8,128)(2,1)}, bf16[1024,256]{1,0:T(8,128)(2,1)}, u32[]{:S(2)}, u32[]{:S(2)}) collective-permute-start(bf16[1024,256]{1,0:T(8,128)(2,1)} %dynamic-slice_bitcast_fusion.1), channel_id=1, source_target_pairs={{0,1},{1,0},{2,3},{3,2},{4,5},{5,4},{6,7},{7,6},{8,9},{9,8},{10,11... | collective-permute-start | bytes 1572872 | tf_op jit(solution)/shard_map/ppermute | solution.py:200
  18.6 16.8 %collective-permute-start.6 = (bf16[8,128,128]{2,1,0:T(8,128)(2,1)S(1)}, bf16[8,128,128]{2,1,0:T(8,128)(2,1)S(1)}, u32[]{:S(2)}, u32[]{:S(2)}) collective-permute-start(bf16[8,128,128]{2,1,0:T(8,128)(2,1)S(1)} %get-tuple-element.35), channel_id=1, source_target_pairs={{0,2},{1,3},{2,0},{3,1},{4,6},{5,7},{6,4},{7,5},{8,10},{9,11},{10,... | collective-permute-start | bytes 786440 | tf_op jit(solution)/shard_map/ppermute | solution.py:200
  20.5 21.1 %collective-permute-start.28 = (bf16[1024,256]{1,0:T(8,128)(2,1)S(1)}, bf16[1024,256]{1,0:T(8,128)(2,1)S(1)}, u32[]{:S(2)}, u32[]{:S(2)}) collective-permute-start(bf16[1024,256]{1,0:T(8,128)(2,1)S(1)} %dynamic-slice_bitcast_fusion), channel_id=1, source_target_pairs={{0,1},{1,0},{2,3},{3,2},{4,5},{5,4},{6,7},{7,6},{8,9},{9,8},{10,11... | collective-permute-start | bytes 1572872 | tf_op jit(solution)/shard_map/ppermute | solution.py:200
  24.1 12.4 %collective-permute-start.24 = (bf16[2,128,128]{2,1,0:T(8,128)(2,1)S(1)}, bf16[2,128,128]{2,1,0:T(8,128)(2,1)S(1)}, u32[]{:S(2)}, u32[]{:S(2)}) collective-permute-start(bf16[2,128,128]{2,1,0:T(8,128)(2,1)S(1)} %get-tuple-element.45), channel_id=1, source_target_pairs={{0,20},{4,16},{8,28},{12,24},{16,4},{20,0},{24,12},{28,8},{1,21},{... | collective-permute-start | bytes 196616 | tf_op jit(solution)/shard_map/ppermute | solution.py:203
  25.4 11.7 %collective-permute-start.25 = (bf16[2,128,128]{2,1,0:T(8,128)(2,1)S(1)}, bf16[2,128,128]{2,1,0:T(8,128)(2,1)S(1)}, u32[]{:S(2)}, u32[]{:S(2)}) collective-permute-start(bf16[2,128,128]{2,1,0:T(8,128)(2,1)S(1)} %get-tuple-element.46), channel_id=1, source_target_pairs={{0,24},{4,28},{8,16},{12,20},{16,8},{20,12},{24,0},{28,4},{1,25},{... | collective-permute-start | bytes 196616 | tf_op jit(solution)/shard_map/ppermute | solution.py:203
  36.5 10.3 %collective-permute-start.1 = (bf16[2,256,256]{2,1,0:T(8,128)(2,1)S(1)}, bf16[2,256,256]{2,1,0:T(8,128)(2,1)S(1)}, u32[]{:S(2)}, u32[]{:S(2)}) collective-permute-start(bf16[2,256,256]{2,1,0:T(8,128)(2,1)S(1)} %get-tuple-element.33.near_ref), channel_id=1, source_target_pairs={{0,2},{1,3},{2,0},{3,1},{4,6},{5,7},{6,4},{7,5},{8,10},{9,11},{10,... | collective-permute-start | bytes 786440 | tf_op jit(solution)/shard_map/ppermute | solution.py:200
  37.7 13.3 %collective-permute-start.27 = (bf16[4,2,128,128]{3,2,1,0:T(8,128)(2,1)S(1)}, bf16[4,2,128,128]{3,2,1,0:T(8,128)(2,1)S(1)}, u32[]{:S(2)}, u32[]{:S(2)}) collective-permute-start(bf16[4,2,128,128]{3,2,1,0:T(8,128)(2,1)S(1)} %shard_map.90), channel_id=1, source_target_pairs={{0,2},{1,3},{2,0},{3,1},{4,6},{5,7},{6,4},{7,5},{8,10},{9,11},{10,... | collective-permute-start | bytes 786440 | tf_op jit(solution)/shard_map/ppermute | solution.py:200
  39.5 11.4 %collective-permute-start.15 = (bf16[2,128,128]{2,1,0:T(8,128)(2,1)S(1)}, bf16[2,128,128]{2,1,0:T(8,128)(2,1)S(1)}, u32[]{:S(2)}, u32[]{:S(2)}) collective-permute-start(bf16[2,128,128]{2,1,0:T(8,128)(2,1)S(1)} %get-tuple-element.40), channel_id=1, source_target_pairs={{0,16},{4,20},{8,24},{12,28},{16,0},{20,4},{24,8},{28,12},{1,17},{... | collective-permute-start | bytes 196616 | tf_op jit(solution)/shard_map/ppermute | solution.py:203
  41.6 12.9 %collective-permute-start.19 = (bf16[2,128,128]{2,1,0:T(8,128)(2,1)S(1)}, bf16[2,128,128]{2,1,0:T(8,128)(2,1)S(1)}, u32[]{:S(2)}, u32[]{:S(2)}) collective-permute-start(bf16[2,128,128]{2,1,0:T(8,128)(2,1)S(1)} %get-tuple-element.42), channel_id=1, source_target_pairs={{0,24},{4,28},{8,16},{12,20},{16,8},{20,12},{24,0},{28,4},{1,25},{... | collective-permute-start | bytes 196616 | tf_op jit(solution)/shard_map/ppermute | solution.py:203
  50.9 10.5 %collective-permute-start.9 = (bf16[2,128,256]{2,1,0:T(8,128)(2,1)S(1)}, bf16[2,128,256]{2,1,0:T(8,128)(2,1)S(1)}, u32[]{:S(2)}, u32[]{:S(2)}) collective-permute-start(bf16[2,128,256]{2,1,0:T(8,128)(2,1)S(1)} %get-tuple-element.37), channel_id=1, source_target_pairs={{0,4},{4,0},{8,12},{12,8},{16,20},{20,16},{24,28},{28,24},{1,5},{5... | collective-permute-start | bytes 393224 | tf_op jit(solution)/shard_map/ppermute | solution.py:203
  50.9 10.6 %collective-permute-start.11 = (bf16[2,128,256]{2,1,0:T(8,128)(2,1)S(1)}, bf16[2,128,256]{2,1,0:T(8,128)(2,1)S(1)}, u32[]{:S(2)}, u32[]{:S(2)}) collective-permute-start(bf16[2,128,256]{2,1,0:T(8,128)(2,1)S(1)} %get-tuple-element.38), channel_id=1, source_target_pairs={{0,8},{4,12},{8,0},{12,4},{16,24},{20,28},{24,16},{28,20},{1,9},{5... | collective-permute-start | bytes 393224 | tf_op jit(solution)/shard_map/ppermute | solution.py:203
  51.1 12.3 %collective-permute-start.13 = (bf16[2,128,256]{2,1,0:T(8,128)(2,1)S(1)}, bf16[2,128,256]{2,1,0:T(8,128)(2,1)S(1)}, u32[]{:S(2)}, u32[]{:S(2)}) collective-permute-start(bf16[2,128,256]{2,1,0:T(8,128)(2,1)S(1)} %get-tuple-element.39), channel_id=1, source_target_pairs={{0,12},{4,8},{8,4},{12,0},{16,28},{20,24},{24,20},{28,16},{1,13},{... | collective-permute-start | bytes 393224 | tf_op jit(solution)/shard_map/ppermute | solution.py:203
  58.7 14.7 %collective-permute-start.8 = (bf16[2,128,256]{2,1,0:T(8,128)(2,1)S(1)}, bf16[2,128,256]{2,1,0:T(8,128)(2,1)S(1)}, u32[]{:S(2)}, u32[]{:S(2)}) collective-permute-start(bf16[2,128,256]{2,1,0:T(8,128)(2,1)S(1)} %get-tuple-element.36.refs_0_), channel_id=1, source_target_pairs={{0,2},{1,3},{2,0},{3,1},{4,6},{5,7},{6,4},{7,5},{8,10},{9,11},{10,... | collective-permute-start | bytes 393224 | tf_op jit(solution)/shard_map/ppermute | solution.py:200
  61.4 12.0 %collective-permute-start.10 = (bf16[2,128,256]{2,1,0:T(8,128)(2,1)S(1)}, bf16[2,128,256]{2,1,0:T(8,128)(2,1)S(1)}, u32[]{:S(2)}, u32[]{:S(2)}) collective-permute-start(bf16[2,128,256]{2,1,0:T(8,128)(2,1)S(1)} %collective-permute-done.9.refs_2_), channel_id=1, source_target_pairs={{0,2},{1,3},{2,0},{3,1},{4,6},{5,7},{6,4},{7,5},{8,10},{9,11},{10,... | collective-permute-start | bytes 393224 | tf_op jit(solution)/shard_map/ppermute | solution.py:200
  61.6 11.9 %collective-permute-start.12 = (bf16[2,128,256]{2,1,0:T(8,128)(2,1)S(1)}, bf16[2,128,256]{2,1,0:T(8,128)(2,1)S(1)}, u32[]{:S(2)}, u32[]{:S(2)}) collective-permute-start(bf16[2,128,256]{2,1,0:T(8,128)(2,1)S(1)} %collective-permute-done.11.refs_4_), channel_id=1, source_target_pairs={{0,2},{1,3},{2,0},{3,1},{4,6},{5,7},{6,4},{7,5},{8,10},{9,11},{10,... | collective-permute-start | bytes 393224 | tf_op jit(solution)/shard_map/ppermute | solution.py:200
  63.5 10.0 %collective-permute-start.14 = (bf16[2,128,256]{2,1,0:T(8,128)(2,1)S(1)}, bf16[2,128,256]{2,1,0:T(8,128)(2,1)S(1)}, u32[]{:S(2)}, u32[]{:S(2)}) collective-permute-start(bf16[2,128,256]{2,1,0:T(8,128)(2,1)S(1)} %collective-permute-done.13.refs_6_), channel_id=1, source_target_pairs={{0,2},{1,3},{2,0},{3,1},{4,6},{5,7},{6,4},{7,5},{8,10},{9,11},{10,... | collective-permute-start | bytes 393224 | tf_op jit(solution)/shard_map/ppermute | solution.py:200
  76.1 41.5 %collective-permute-start.29 = (bf16[1024,1024]{1,0:T(8,128)(2,1)S(1)}, bf16[1024,1024]{1,0:T(8,128)(2,1)S(1)}, u32[]{:S(2)}, u32[]{:S(2)}) collective-permute-start(bf16[1024,1024]{1,0:T(8,128)(2,1)S(1)} %get-tuple-element.48.grad_ref), channel_id=1, source_target_pairs={{0,1},{1,0},{2,3},{3,2},{4,5},{5,4},{6,7},{7,6},{8,9},{9,8},{10,11... | collective-permute-start | bytes 6291464 | tf_op jit(solution)/shard_map/ppermute | solution.py:200
  78.4 12.6 %collective-permute-start.30 = (bf16[2,256,256]{2,1,0:T(8,128)(2,1)S(1)}, bf16[2,256,256]{2,1,0:T(8,128)(2,1)S(1)}, u32[]{:S(2)}, u32[]{:S(2)}) collective-permute-start(bf16[2,256,256]{2,1,0:T(8,128)(2,1)S(1)} %get-tuple-element.51.near_ref), channel_id=1, source_target_pairs={{0,2},{1,3},{2,0},{3,1},{4,6},{5,7},{6,4},{7,5},{8,10},{9,11},{10,... | collective-permute-start | bytes 786440 | tf_op jit(solution)/shard_map/ppermute | solution.py:200
  79.4 14.2 %collective-permute-start.38 = (bf16[2,128,256]{2,1,0:T(8,128)(2,1)S(1)}, bf16[2,128,256]{2,1,0:T(8,128)(2,1)S(1)}, u32[]{:S(2)}, u32[]{:S(2)}) collective-permute-start(bf16[2,128,256]{2,1,0:T(8,128)(2,1)S(1)} %get-tuple-element.61), channel_id=1, source_target_pairs={{0,24},{4,28},{8,16},{12,20},{16,8},{20,12},{24,0},{28,4},{1,25},{... | collective-permute-start | bytes 393224 | tf_op jit(solution)/shard_map/ppermute | solution.py:203
  79.6 22.5 %collective-permute-start.32 = (bf16[2,256,256]{2,1,0:T(8,128)(2,1)S(1)}, bf16[2,256,256]{2,1,0:T(8,128)(2,1)S(1)}, u32[]{:S(2)}, u32[]{:S(2)}) collective-permute-start(bf16[2,256,256]{2,1,0:T(8,128)(2,1)S(1)} %get-tuple-element.55.near_ref), channel_id=1, source_target_pairs={{0,2},{1,3},{2,0},{3,1},{4,6},{5,7},{6,4},{7,5},{8,10},{9,11},{10,... | collective-permute-start | bytes 786440 | tf_op jit(solution)/shard_map/ppermute | solution.py:200
  101.6 14.5 %collective-permute-start.40 = (bf16[5,128,256]{2,1,0:T(8,128)(2,1)S(1)}, bf16[5,128,256]{2,1,0:T(8,128)(2,1)S(1)}, u32[]{:S(2)}, u32[]{:S(2)}) collective-permute-start(bf16[5,128,256]{2,1,0:T(8,128)(2,1)S(1)} %shard_map.97), channel_id=1, source_target_pairs={{0,1},{1,0},{2,3},{3,2},{4,5},{5,4},{6,7},{7,6},{8,9},{9,8},{10,11... | collective-permute-start | bytes 983048 | tf_op jit(solution)/shard_map/ppermute | solution.py:200
  103.5 11.2 %collective-permute-start.34 = (bf16[2,128,256]{2,1,0:T(8,128)(2,1)S(1)}, bf16[2,128,256]{2,1,0:T(8,128)(2,1)S(1)}, u32[]{:S(2)}, u32[]{:S(2)}) collective-permute-start(bf16[2,128,256]{2,1,0:T(8,128)(2,1)S(1)} %get-tuple-element.57), channel_id=1, source_target_pairs={{0,12},{4,8},{8,4},{12,0},{16,28},{20,24},{24,20},{28,16},{1,13},{... | collective-permute-start | bytes 393224 | tf_op jit(solution)/shard_map/ppermute | solution.py:203
  (26 other events, 177.4 us)
